TPU v7x, 256 devices: a whole 4x4x8 slice. The times are simulated.
256 devices in a mesh: dp: 8 (over y, core), head: 2 (over z_lo), kv: 16 (over z_hi, x).
Axes of the slice: x: 4, y: 4, z: 8 (z_hi: 4, z_lo: 2; z = z_hi * 2 + z_lo), core: 2. Of those that a mesh axis runs over, the one named last changes fastest.
Arguments:
- teacher_query: bfloat16 [8, 4096, 3584], P('dp', 'kv', 'head'), may hold values from -96 to 96
- teacher_key: bfloat16 [8, 4096, 512], P('dp', 'kv', 'head'), may hold values from -8 to 8
- student_query: bfloat16 [8, 4096, 1792], P('dp', 'kv', 'head'), may hold values from -96 to 96
- student_key: bfloat16 [8, 4096, 256], P('dp', 'kv', 'head'), may hold values from -8 to 8
- pair_table: int32 [14, 2], replicated, may hold values from 0 to 27, as said below
Outputs:
- kl: float32 [8, 14, 4096], P('dp', 'head', 'kv')
- head_loss: float32 [14], P('head')
Inputs may be any that keep to these rules, and one draw needn't show every extreme that they name: `pair_table`: each of the 28 teacher heads appears exactly once in the table.
All inputs are finite; a program needn't handle non-finite values.
Results may differ from a plain program's by a relative error of at most 0.0003.
Values may be sent and summed in bfloat16 or wider, within the bound.
No kernel may reach another device: no remote copies, remote signals or barrier semaphores. Data moves between devices by JAX's collectives and lax.ppermute only.
A program may use at most 64 MiB of HBM per device.

v0:
```python
import math
import jax
import jax.numpy as jnp
from jax import lax
from jax.sharding import Mesh
from jax.sharding import PartitionSpec as P

HT = 28
KVT = 4
DH = 128
HS = 14
KVS = 2
KV = ("kv_0", "kv_1")
DP = ("dp_0", "dp_1")
DP_KV = ("dp_0", "dp_1", "kv_0", "kv_1")
masked_value = -1e30


def from_everyone(shard, axis):
    count = lax.axis_size(axis)
    return lax.all_to_all(
        jnp.broadcast_to(shard[None], (count, *shard.shape)), axis, 0, 0, tiled=True
    )


def joined_along(blocks, dim):
    dims = list(blocks.shape[1:])
    dims[dim] *= blocks.shape[0]
    return jnp.moveaxis(blocks, 0, dim).reshape(dims)


def gathered_copies(shard, axis, dim):
    blocks = from_everyone(shard, axis)
    return joined_along(blocks, dim)


def one_axis_at_a_time(shard, axes):
    for axis in axes:
        shard = lax.psum(shard, axis)
    return shard


def running_softmax(running_max, running_total, logits, causal_mask):
    filled = jnp.where(causal_mask, logits, masked_value)
    new_max = jnp.maximum(running_max, jnp.max(filled, axis=-1))
    rescale = jnp.exp(running_max - new_max)
    weights = jnp.where(causal_mask, jnp.exp(filled - new_max[..., None]), 0.0)
    return (new_max, running_total * rescale + jnp.sum(weights, axis=-1), rescale, weights)


def make_fold(teacher_heads, teacher_select, student_heads, student_select, repeat, query_pos):
    seq_dev, row_count, pair_count, head_dim = teacher_heads.shape
    student_count = student_heads.shape[2]
    scale = 1.0 / math.sqrt(head_dim)
    last_query = query_pos[row_count - 1]

    def fold_step(carry, pieces, start):
        teacher_keys, student_keys = pieces
        key_count = teacher_keys.shape[1]
        block_size = math.gcd(key_count, 512)
        block_total = key_count // block_size
        visible = jnp.clip(last_query // block_size + 1, 0, block_total)

        def one_block(block_index, state):
            t_max, t_total, t_cross, s_max, s_total = state
            offset = block_index * block_size
            t_block = lax.dynamic_slice_in_dim(teacher_keys, offset, block_size, 1).reshape(
                seq_dev, block_size, -1, head_dim
            )
            s_block = lax.dynamic_slice_in_dim(student_keys, offset, block_size, 1).reshape(
                seq_dev, block_size, -1, head_dim
            )
            t_keys = jnp.take(t_block, teacher_select, axis=2)
            s_keys = jnp.take(s_block, student_select, axis=2)
            t_logits = (
                jnp.einsum(
                    "bqpd,bkpd->bpqk", teacher_heads, t_keys, preferred_element_type=jnp.float32
                )
                * scale
            )
            s_logits = (
                jnp.einsum(
                    "bqsd,bksd->bsqk", student_heads, s_keys, preferred_element_type=jnp.float32
                )
                * scale
            )
            key_pos = offset + jnp.arange(block_size, dtype=jnp.int32)
            causal_mask = key_pos[None, :] <= query_pos[:, None]
            t_max, t_total, t_rescale, t_weights = running_softmax(
                t_max, t_total, t_logits, causal_mask
            )
            s_max, s_total, s_rescale, s_weights = running_softmax(
                s_max, s_total, s_logits, causal_mask
            )
            split_logits = t_logits.reshape(seq_dev, student_count, repeat, row_count, block_size)
            gap = (split_logits - s_logits[:, :, None]).reshape(
                seq_dev, pair_count, row_count, block_size
            )
            t_cross = t_cross * t_rescale + jnp.sum(t_weights * gap, axis=-1)
            return (t_max, t_total, t_cross, s_max, s_total)

        return lax.fori_loop(0, visible, one_block, carry)

    pair_shape = (seq_dev, pair_count, row_count)
    student_shape = (seq_dev, student_count, row_count)
    initial = (
        jnp.full(pair_shape, masked_value, jnp.float32),
        jnp.zeros(pair_shape, jnp.float32),
        jnp.zeros(pair_shape, jnp.float32),
        jnp.full(student_shape, masked_value, jnp.float32),
        jnp.zeros(student_shape, jnp.float32),
    )
    return (fold_step, initial)


def finish_pairs(state, repeat):
    t_max, t_total, t_cross, s_max, s_total = state
    seq_dev, pair_count, row_count = t_max.shape
    student_count = s_max.shape[1]
    t_lse = t_max + jnp.log(t_total)
    s_lse = s_max + jnp.log(s_total)
    s_paired = jnp.broadcast_to(
        s_lse[:, :, None], (seq_dev, student_count, repeat, row_count)
    ).reshape(seq_dev, pair_count, row_count)
    return t_cross / t_total - t_lse + s_paired


def per_device(teacher_query, teacher_key, student_query, student_key, pair_table):
    seq_dev, row_count, teacher_width = teacher_query.shape
    n_head = lax.axis_size("head")
    n_kv = lax.axis_size(KV)
    n_data = lax.axis_size(DP)
    head_index = lax.axis_index("head")
    kv_index = lax.axis_index(KV)
    group_teacher = HT // KVT
    group_student = HS // KVS
    local_student = HS // n_head
    local_student_kv = KVS // n_head
    query_pos = kv_index * row_count + jnp.arange(row_count, dtype=jnp.int32)
    all_tq, all_tk = (
        gathered_copies(teacher_query, "head", 2),
        gathered_copies(teacher_key, "head", 2),
    )
    my_pairs = lax.dynamic_slice_in_dim(
        pair_table, head_index * local_student, local_student, 0
    ).reshape(-1)
    teacher_heads = jnp.take(all_tq.reshape(seq_dev, row_count, HT, DH), my_pairs, axis=2)
    teacher_select = my_pairs // group_teacher
    student_heads = student_query.reshape(seq_dev, row_count, local_student, DH)
    student_ids = head_index * local_student + jnp.arange(local_student, dtype=jnp.int32)
    student_select = student_ids // group_student - head_index * local_student_kv
    fold_step, initial = make_fold(
        teacher_heads, teacher_select, student_heads, student_select, 2, query_pos
    )
    state = fold_step(
        initial,
        (
            lax.all_gather(all_tk, KV, axis=1, tiled=True),
            lax.all_gather(student_key, KV, axis=1, tiled=True),
        ),
        jnp.int32(0),
    )
    pair_kl = finish_pairs(state, 2)
    kl_local = jnp.sum(pair_kl.reshape(seq_dev, local_student, 2, row_count), axis=2)
    head_sums = jnp.sum(kl_local, axis=(0, 2))
    total = one_axis_at_a_time(head_sums, DP_KV)
    head_loss = total / (seq_dev * n_data * row_count * n_kv)
    return (kl_local, head_loss)


def solution(mesh):
    split = Mesh(
        mesh.devices.reshape(4, 2, mesh.shape["head"], 4, 4),
        ("dp_0", "dp_1", "head", "kv_0", "kv_1"),
    )
    in_specs = (P(DP, KV, "head"), P(DP, KV, "head"), P(DP, KV, "head"), P(DP, KV, "head"), P())
    out_specs = (P(DP, "head", KV), P("head"))
    return jax.shard_map(
        per_device, mesh=split, in_specs=in_specs, out_specs=out_specs, check_vma=False
    )
```

profile of v0, /device:TPU:0, one launch (start us, length us, event | category | flops | bytes accessed | tf_op | source)
XLA Modules:
  0.0 263.1 jit_solution(12517146968400585087)
XLA Ops:
  7.2 0.0 copy-start
  7.2 0.0 all-gather.5.cloned.1.call-start
  7.2 0.7 all-gather.5.cloned.1.call-update
  7.9 0.0 all-gather.3.cloned.1.call-start
  8.0 1.0 copy.25
  9.0 8.2 %all_to_all.10 = bf16[2,1,256,256]{2,3,1,0:T(8,128)(2,1)} all-to-all(bf16[2,1,256,256]{2,3,1,0:T(8,128)(2,1)S(1)} %broadcast_in_dim.98), channel_id=1, replica_groups=mesh['dp_0'=4,'dp_1'=2,'head'=2,'kv_0'=4,'kv_1'=4] {'head'}, dimensions={0} | all-to-all | bytes 524288 | tf_op jit(solution)/shard_map/all_to_all | solution.py:21
  17.2 0.0 all-gather.3.cloned.1.call-update
  17.3 1.5 copy.26
  18.7 0.0 copy-start.1
  18.7 1.4 broadcast_in_dim.101
  20.1 3.7 %all-to-all-start.1 = ((bf16[2,1,256,1792]{2,3,1,0:T(8,128)(2,1)}), bf16[2,1,256,1792]{2,3,1,0:T(8,128)(2,1)S(1)}, u32[]{:S(2)}, u32[]{:S(2)}) async-start(bf16[2,1,256,1792]{2,3,1,0:T(8,128)(2,1)} %broadcast_in_dim.101), calls=%async_computation.1 | async-start | bytes 3670016 | tf_op jit(solution)/shard_map/all_to_all | solution.py:21
  23.9 0.6 slice.3
  26.4 0.0 copy-done
  26.4 0.1 constant_dynamic-slice_fusion.1
  26.5 0.1 copy.24
  26.6 0.1 reshape.178
  26.7 0.1 reshape.180
  27.4 0.0 copy-done.1
  27.4 0.2 copy.30
  27.6 1.0 copy.31
  28.7 16.9 %all-to-all-done.1 = bf16[2,1,256,1792]{2,3,1,0:T(8,128)(2,1)S(1)} async-done(((bf16[2,1,256,1792]{2,3,1,0:T(8,128)(2,1)}), bf16[2,1,256,1792]{2,3,1,0:T(8,128)(2,1)S(1)}, u32[]{:S(2)}, u32[]{:S(2)}) %all-to-all-start.1) | async-done | bytes 1835040 | tf_op jit(solution)/shard_map/all_to_all | solution.py:21
  45.6 2.6 copy.29
  48.2 2.2 gather_fusion.1
  50.4 0.1 bitcast_select_fusion.1
  50.6 15.0 %all-gather.5.cloned.1.call-done = bf16[1,4096,128]{2,1,0:T(8,128)(2,1)} async-done(((bf16[1,256,128]{2,1,0:T(8,128)(2,1)}), bf16[1,4096,128]{2,1,0:T(8,128)(2,1)}) %all-gather.5.cloned.1.call-update) | async-done | bytes 1048592 | tf_op jit(solution)/shard_map/all_gather | solution.py:159
  65.5 81.5 %all-gather.3.cloned.1.call-done = bf16[1,4096,512]{1,2,0:T(8,128)(2,1)} async-done(((bf16[1,256,512]{1,2,0:T(8,128)(2,1)}), bf16[1,4096,512]{1,2,0:T(8,128)(2,1)}) %all-gather.3.cloned.1.call-update) | async-done | bytes 4194320 | tf_op jit(solution)/shard_map/all_gather | solution.py:158
  147.1 9.1 %while.19 = (s32[]{:T(128)}, f32[1,14,256]{2,1,0:T(8,128)S(1)}, f32[1,14,256]{2,1,0:T(8,128)S(1)}, f32[1,14,256]{2,1,0:T(8,128)S(1)}, f32[1,7,256]{2,1,0:T(8,128...) while((s32[]{:T(128)}, f32[1,14,256]{2,1,0:T(8,128)S(1)}, ...), condition=%wide.region_6.7_spmd.clone, body=%wide.region_0.6_spmd.clone.sunk | while | flops 732774400 | bytes 37899856 | solution.py:102
  147.1 1.1 constant_dynamic-slice_fusion.3
  148.2 0.3 copy.33
  148.5 0.9 gather_fusion
  149.4 0.1 broadcast_compare_fusion.2
  149.6 0.0 copy-start.2
  149.6 1.4 fusion.28
  151.0 0.9 dynamic-slice_bitcast_fusion.2
  152.0 0.0 copy-done.2
  152.0 0.8 select_reduce_fusion.4
  152.8 2.6 fusion.29
  155.4 0.8 select_reduce_fusion.5
  156.3 0.1 fusion.23
  156.4 0.1 reduce_sum.63
  156.5 0.1 reduce_sum.64
  156.6 10.3 %psum.28 = f32[7]{0:T(128)S(1)} all-reduce(f32[7]{0:T(128)S(1)} %reduce_sum.64), channel_id=1, replica_groups=mesh['dp_0'=4,'dp_1'=2,'head'=2,'kv_0'=4,'kv_1'=4] {'dp_0'}, use_global_device_ids=true, to_apply=%region_10.11 | all-reduce | flops 7 | bytes 56 | tf_op jit(solution)/shard_map/psum | solution.py:39
  166.9 2.5 psum.29
  169.4 65.0 %psum.30 = f32[7]{0:T(128)S(1)} all-reduce(f32[7]{0:T(128)S(1)} %psum.29), channel_id=1, replica_groups=mesh['dp_0'=4,'dp_1'=2,'head'=2,'kv_0'=4,'kv_1'=4] {'kv_0'}, use_global_device_ids=true, to_apply=%region_12.13 | all-reduce | flops 7 | bytes 56 | tf_op jit(solution)/shard_map/psum | solution.py:39
  234.4 0.6 reduce_sum.61
  235.0 20.8 %psum.31 = f32[7]{0:T(128)S(1)} all-reduce(f32[7]{0:T(128)S(1)} %psum.30), channel_id=1, replica_groups=mesh['dp_0'=4,'dp_1'=2,'head'=2,'kv_0'=4,'kv_1'=4] {'kv_1'}, use_global_device_ids=true, to_apply=%region_13.14 | all-reduce | flops 7 | bytes 56 | tf_op jit(solution)/shard_map/psum | solution.py:39
  255.8 0.5 broadcast_multiply_fusion
  (28 shorter events, 0.2 us)
Async XLA Ops:
  7.2 19.2 %copy-start = (s32[14,2]{0,1:T(2,128)S(1)}, s32[14,2]{0,1:T(2,128)}, u32[]{:S(2)}) copy-start(s32[14,2]{0,1:T(2,128)} %param.11) | copy-start | bytes 340
  7.2 58.3 %all-gather.5.cloned.1.call-start = ((), (), s32[]{:S(2)}) async-start(), calls=%async_computation.3 | async-start | bytes 1114112 | tf_op jit(solution)/shard_map/all_gather | solution.py:159
  7.9 139.1 %all-gather.3.cloned.1.call-start = ((), (), s32[]{:S(2)}) async-start(), calls=%async_computation.2 | async-start | bytes 4456448 | tf_op jit(solution)/shard_map/all_gather | solution.py:158
  18.7 8.7 %copy-start.1 = (bf16[1,256,896]{2,1,0:T(8,128)(2,1)S(1)}, bf16[1,256,896]{2,1,0:T(8,128)(2,1)}, u32[]{:S(2)}) copy-start(bf16[1,256,896]{2,1,0:T(8,128)(2,1)} %param.9) | copy-start | bytes 1376260
  20.1 25.4 %all-to-all-start.1 = ((bf16[2,1,256,1792]{2,3,1,0:T(8,128)(2,1)}), bf16[2,1,256,1792]{2,3,1,0:T(8,128)(2,1)S(1)}, u32[]{:S(2)}, u32[]{:S(2)}) async-start(bf16[2,1,256,1792]{2,3,1,0:T(8,128)(2,1)} %broadcast_in_dim.101), calls=%async_computation.1 | async-start | bytes 3670016 | tf_op jit(solution)/shard_map/all_to_all | solution.py:21
  149.6 2.4 copy-start.2
Sparse Core Ops, SparseCore 0:
  10.4 55.0 all-gather.4
  67.9 79.0 all-gather.2
where the time goes:
time: 264 us; the launch traced here: 263 us
  waiting for transfers between devices  114 us (43%)
  blocking collectives  107 us (41%)
  between operations  16.8 us (6%)
  local copies, waits for them, and re-layouts  14.7 us (6%)
  other arithmetic  4.56 us (2%)
  starting transfers between devices  3.79 us (1%)
    psum x4, blocking collectives, one_axis_at_a_time(): shard = lax.psum(shard, axis)  98.5 us
    all_gather x1, waiting for transfers between devices, per_device(): lax.all_gather(all_tk, KV, axis=1, tiled=True)  81.5 us
    all_to_all x1, waiting for transfers between devices, from_everyone(): lax.all_to_all(jnp.broadcast_to(shard[None], (count, *shard.shape)), axis...  16.9 us
    all_gather x1, waiting for transfers between devices, per_device(): lax.all_gather(student_key, KV, axis=1, tiled=True)  15 us
    all_to_all x1, blocking collectives, from_everyone(): lax.all_to_all(jnp.broadcast_to(shard[None], (count, *shard.shape)), axis...  8.25 us
  transfers between devices with their start and end apart: 3, of which 3 were waited for; matrix products, arithmetic and copies ran while one was open for 4% of the time, Pallas kernels for 0%

commit v1 on v0

--- a/solution.py
+++ b/solution.py
@@ -156,7 +156,9 @@
         initial,
         (
             lax.all_gather(all_tk, KV, axis=1, tiled=True),
-            lax.all_gather(student_key, KV, axis=1, tiled=True),
+            jnp.concatenate(
+                lax.all_to_all(jnp.stack([student_key] * lax.axis_size(KV)), KV, 0, 0), axis=1
+            ),
         ),
         jnp.int32(0),
     )

time: 264 us -> 245 us (0.928)
  waiting for transfers between devices: 114 us -> 47.4 us
  blocking collectives: 107 us -> 140 us
  starting transfers between devices: 3.79 us -> 14.2 us
    all_gather x1, waiting for transfers between devices: 81.5 us -> 17.4 us  [per_device(): lax.all_gather(all_tk, KV, axis=1, tiled=True)]
    all_to_all x1 -> x2, blocking collectives: 8.25 us -> 36 us  [from_everyone(): lax.all_to_all(jnp.broadcast_to(shard[None], (count, *shard.shape)), axis...]
    all_gather x1 -> x0, waiting for transfers between devices: 15 us -> none  [per_device(): lax.all_gather(student_key, KV, axis=1, tiled=True)]
    all_to_all x1, waiting for transfers between devices: 16.9 us -> 30 us  [per_device(): lax.all_to_all(jnp.stack([student_key] * lax.axis_size(KV)), KV, 0, 0)]
    all_to_all x1, starting transfers between devices: 3.72 us -> 14.2 us  [per_device(): lax.all_to_all(jnp.stack([student_key] * lax.axis_size(KV)), KV, 0, 0)]
    psum x4, blocking collectives: 98.5 us -> 104 us  [one_axis_at_a_time(): shard = lax.psum(shard, axis)]
  transfers between devices with their start and end apart: 3 -> 2, of which waited for: 3 -> 2; matrix products, arithmetic and copies ran while one was open for 4% -> 5% of each run, Pallas kernels for 0% -> 0%
where the time goes in v1:
time: 245 us; the launch traced here: 243 us
  blocking collectives  140 us (57%)
  waiting for transfers between devices  47.4 us (19%)
  between operations  16.8 us (7%)
  local copies, waits for them, and re-layouts  14.8 us (6%)
  starting transfers between devices  14.2 us (6%)
  other arithmetic  5.5 us (2%)
  matrix products  3.43 us (1%)
    psum x4, blocking collectives, one_axis_at_a_time(): shard = lax.psum(shard, axis)  104 us
    all_to_all x2, blocking collectives, from_everyone(): lax.all_to_all(jnp.broadcast_to(shard[None], (count, *shard.shape)), axis...  36 us
    all_to_all x1, waiting for transfers between devices, per_device(): lax.all_to_all(jnp.stack([student_key] * lax.axis_size(KV)), KV, 0, 0)  30 us
    all_gather x1, waiting for transfers between devices, per_device(): lax.all_gather(all_tk, KV, axis=1, tiled=True)  17.4 us
    all_to_all x1, starting transfers between devices, per_device(): lax.all_to_all(jnp.stack([student_key] * lax.axis_size(KV)), KV, 0, 0)  14.2 us
  transfers between devices with their start and end apart: 2, of which 2 were waited for; matrix products, arithmetic and copies ran while one was open for 5% of the time, Pallas kernels for 0%

profile of v1, /device:TPU:0, one launch (start us, length us, event | category | flops | bytes accessed | tf_op | source)
XLA Modules:
  0.0 242.5 jit_solution(11975710500207430732)
XLA Ops:
  7.2 0.0 copy-start
  7.2 0.0 all-gather.2.cloned.1.call-start
  7.2 1.0 copy.25
  8.3 8.2 %all_to_all.15 = bf16[2,1,256,256]{2,3,1,0:T(8,128)(2,1)} all-to-all(bf16[2,1,256,256]{2,3,1,0:T(8,128)(2,1)S(1)} %broadcast_in_dim.98), channel_id=1, replica_groups=mesh['dp_0'=4,'dp_1'=2,'head'=2,'kv_0'=4,'kv_1'=4] {'head'}, dimensions={0} | all-to-all | bytes 524288 | tf_op jit(solution)/shard_map/all_to_all | solution.py:21
  16.5 0.0 all-gather.2.cloned.1.call-update
  16.5 1.5 copy.26
  18.0 0.0 copy-start.2
  18.0 0.1 broadcast_in_dim.101
  18.1 27.8 %all_to_all.16 = bf16[2,1,256,1792]{2,3,1,0:T(8,128)(2,1)S(1)} all-to-all(bf16[2,1,256,1792]{2,3,1,0:T(8,128)(2,1)S(1)} %broadcast_in_dim.101), channel_id=1, replica_groups=mesh['dp_0'=4,'dp_1'=2,'head'=2,'kv_0'=4,'kv_1'=4] {'head'}, dimensions={0} | all-to-all | bytes 3670016 | tf_op jit(solution)/shard_map/all_to_all | solution.py:21
  45.9 0.0 copy-done.2
  45.9 1.2 stack.2
  47.1 14.2 %all-to-all-start.2 = ((bf16[16,1,256,128]{3,2,1,0:T(8,128)(2,1)}), bf16[16,1,256,128]{3,2,1,0:T(8,128)(2,1)S(1)}, u32[]{:S(2)}, u32[]{:S(2)}) async-start(bf16[16,1,256,128]{3,2,1,0:T(8,128)(2,1)} %stack.2), calls=%async_computation.2 | async-start | bytes 2097152 | tf_op jit(solution)/shard_map/all_to_all | solution.py:160
  61.3 0.6 slice.3
  63.9 0.0 copy-done
  63.9 0.1 constant_dynamic-slice_fusion.1
  63.9 0.1 copy.24
  64.0 0.1 reshape.184
  64.1 0.1 reshape.186
  64.9 1.2 copy.30
  66.1 1.0 copy.31
  67.1 2.6 %copy.29 = bf16[256,28,128]{2,0,1:T(8,128)(2,1)} copy(bf16[256,28,128]{0,2,1:T(8,128)(2,1)S(1)} %bitcast.108) | data formatting | bytes 3670016 | tf_op jit(solution)/shard_map/reshape;reshape | solution.py:147
  69.7 2.2 gather_fusion.1
  72.0 1.1 bitcast_select_fusion.1
  73.1 30.0 %all-to-all-done.2 = bf16[16,1,256,128]{3,2,1,0:T(8,128)(2,1)S(1)} async-done(((bf16[16,1,256,128]{3,2,1,0:T(8,128)(2,1)}), bf16[16,1,256,128]{3,2,1,0:T(8,128)(2,1)S(1)}, u32[]{:S(2)}, u32[]{:S(2)}) %all-to-all-start.2) | async-done | bytes 1048608 | tf_op jit(solution)/shard_map/all_to_all | solution.py:160
  103.0 17.4 %all-gather.2.cloned.1.call-done = bf16[1,4096,512]{1,2,0:T(8,128)(2,1)} async-done(((bf16[1,256,512]{1,2,0:T(8,128)(2,1)}), bf16[1,4096,512]{1,2,0:T(8,128)(2,1)}) %all-gather.2.cloned.1.call-update) | async-done | bytes 4194320 | tf_op jit(solution)/shard_map/all_gather | solution.py:158
  120.5 9.5 %while.19 = (s32[]{:T(128)}, f32[1,14,256]{2,1,0:T(8,128)S(1)}, f32[1,14,256]{2,1,0:T(8,128)S(1)}, f32[1,14,256]{2,1,0:T(8,128)S(1)}, f32[1,7,256]{2,1,0:T(8,128...) while((s32[]{:T(128)}, f32[1,14,256]{2,1,0:T(8,128)S(1)}, ...), condition=%wide.region_6.7_spmd.clone, body=%wide.region_0.6_spmd.clone.sunk | while | flops 732774400 | bytes 37899856 | solution.py:102
  120.5 1.1 constant_dynamic-slice_fusion.3
  121.6 0.3 copy.33
  121.9 0.9 gather_fusion
  122.8 0.1 broadcast_compare_fusion.2
  123.0 0.0 copy-start.1
  123.0 2.6 %fusion.28 = (f32[14,256]{1,0:T(8,128)S(1)}, f32[14,512,256]{2,1,0:T(8,128)S(1)}) fusion(pred[256,512]{0,1:T(8,128)(4,1)S(1)} %broadcast_compare_fusion.2, bf16[1,256,14,128]{3,1,2,0:T(8,128)(2,1)} %get-tuple-element.361, bf16[14,512,128]{2,1,0:T(8,128)(2,1)S(1)} %gather_fusion, pred[14]{0:T(512)(128)(4,1)S(1)} %compare_and_fusion.5), kind=kOutput, calls=%fused_computation.9.clone.1 | convolution fusion | flops 476180992 | bytes 10237966 | tf_op jit(solution)/shard_map/while/body/bqpd,bkpd->bpqk/dot_general | solution.py:76
  125.7 0.0 copy-done.1
  125.7 0.8 select_reduce_fusion.4
  126.5 2.6 %fusion.29 = (f32[14,256]{1,0:T(8,128)S(1)}, f32[14,256]{1,0:T(8,128)S(1)}) fusion(f32[14,512,256]{2,1,0:T(8,128)S(1)} %get-tuple-element.307, f32[7,256,512]{1,2,0:T(8,128)S(1)} %get-tuple-element.308, f32[14,256]{1,0:T(8,128)S(1)} %bitcast.109, pred[256,512]{0,1:T(8,128)(4,1)S(1)} %broadcast_compare_fusion.2), kind=kLoop, calls=%fused_computation.6.clone.1 | loop fusion | flops 14672896 | bytes 11184128 | tf_op jit(solution)/shard_map/while/body/reduce_sum | solution.py:99
  129.2 0.8 select_reduce_fusion.5
  130.0 0.1 fusion.23
  130.2 0.1 reduce_sum.63
  130.2 0.1 reduce_sum.64
  130.4 10.5 %psum.28 = f32[7]{0:T(128)S(1)} all-reduce(f32[7]{0:T(128)S(1)} %reduce_sum.64), channel_id=1, replica_groups=mesh['dp_0'=4,'dp_1'=2,'head'=2,'kv_0'=4,'kv_1'=4] {'dp_0'}, use_global_device_ids=true, to_apply=%region_10.11 | all-reduce | flops 7 | bytes 56 | tf_op jit(solution)/shard_map/psum | solution.py:39
  140.9 2.5 %psum.29 = f32[7]{0:T(128)S(1)} all-reduce(f32[7]{0:T(128)S(1)} %psum.28), channel_id=1, replica_groups=mesh['dp_0'=4,'dp_1'=2,'head'=2,'kv_0'=4,'kv_1'=4] {'dp_1'}, use_global_device_ids=true, to_apply=%region_11.12 | all-reduce | flops 7 | bytes 56 | tf_op jit(solution)/shard_map/psum | solution.py:39
  143.3 72.3 %psum.30 = f32[7]{0:T(128)S(1)} all-reduce(f32[7]{0:T(128)S(1)} %psum.29), channel_id=1, replica_groups=mesh['dp_0'=4,'dp_1'=2,'head'=2,'kv_0'=4,'kv_1'=4] {'kv_0'}, use_global_device_ids=true, to_apply=%region_12.13 | all-reduce | flops 7 | bytes 56 | tf_op jit(solution)/shard_map/psum | solution.py:39
  215.7 0.6 reduce_sum.61
  216.3 18.9 %psum.31 = f32[7]{0:T(128)S(1)} all-reduce(f32[7]{0:T(128)S(1)} %psum.30), channel_id=1, replica_groups=mesh['dp_0'=4,'dp_1'=2,'head'=2,'kv_0'=4,'kv_1'=4] {'kv_1'}, use_global_device_ids=true, to_apply=%region_13.14 | all-reduce | flops 7 | bytes 56 | tf_op jit(solution)/shard_map/psum | solution.py:39
  235.2 0.5 broadcast_multiply_fusion
  (29 shorter events, 0.2 us)
Async XLA Ops:
  7.2 56.7 %copy-start = (s32[14,2]{0,1:T(2,128)S(1)}, s32[14,2]{0,1:T(2,128)}, u32[]{:S(2)}) copy-start(s32[14,2]{0,1:T(2,128)} %param.11) | copy-start | bytes 340
  7.2 113.3 %all-gather.2.cloned.1.call-start = ((), (), s32[]{:S(2)}) async-start(), calls=%async_computation.3 | async-start | bytes 4456448 | tf_op jit(solution)/shard_map/all_gather | solution.py:158
  18.0 27.9 %copy-start.2 = (bf16[1,256,128]{2,1,0:T(8,128)(2,1)S(1)}, bf16[1,256,128]{2,1,0:T(8,128)(2,1)}, u32[]{:S(2)}) copy-start(bf16[1,256,128]{2,1,0:T(8,128)(2,1)} %param.10) | copy-start | bytes 196612
  47.1 55.9 %all-to-all-start.2 = ((bf16[16,1,256,128]{3,2,1,0:T(8,128)(2,1)}), bf16[16,1,256,128]{3,2,1,0:T(8,128)(2,1)S(1)}, u32[]{:S(2)}, u32[]{:S(2)}) async-start(bf16[16,1,256,128]{3,2,1,0:T(8,128)(2,1)} %stack.2), calls=%async_computation.2 | async-start | bytes 2097152 | tf_op jit(solution)/shard_map/all_to_all | solution.py:160
  123.0 2.7 %copy-start.1 = (bf16[1,256,7,128]{3,1,2,0:T(8,128)(2,1)S(1)}, bf16[1,256,7,128]{3,1,2,0:T(8,128)(2,1)}, u32[]{:S(2)}) copy-start(bf16[1,256,7,128]{3,1,2,0:T(8,128)(2,1)} %get-tuple-element.363) | copy-start | bytes 1376260 | tf_op jit(solution)/shard_map/while
Sparse Core Ops, SparseCore 0:
  16.7 103.7 all-gather.1
